TPU v7x, 32 devices: a whole 2x2x4 slice. The times are simulated.
32 devices in a mesh: grp: 2 (over x), tp: 4 (over y, core), pp: 4 (over z).
Axes of the slice: x: 2, y: 2, z: 4, core: 2. Of those that a mesh axis runs over, the one named last changes fastest.
Arguments:
- tokens: bfloat16 [1024, 8192], P('grp', 'tp'), parts along dimension 0, may hold values from -12 to 12
- gain: bfloat16 [4, 8192], P('pp', 'tp'), may hold values from 0.099609375 to 1.8984375
- q_weight: bfloat16 [4, 8192, 4096], P('pp', None, 'tp'), may hold values from -0.5 to 0.5
- kv_weight: bfloat16 [4, 8192, 2048], P('pp', None, 'tp'), may hold values from -0.5 to 0.5
- out_weight: bfloat16 [4, 4096, 8192], P('pp', None, 'tp'), may hold values from -0.09375 to 0.09375
- page_table: int32 [4, 8, 128], P('pp'), may hold values from 0 to 1023, as said below
- segment_ids: int32 [1024], P('grp'), parts along dimension 0, may hold values from 0 to 2, never falling along the last dimension, each value on 1 to 256 neighbouring positions
Outputs:
- hidden: bfloat16 [1024, 8192], P(('grp', 'pp'), 'tp'), parts along dimension 0
- kv_cache: bfloat16 [4, 2048, 4, 256], P('pp', ('grp', 'tp')), parts along dimension 1
There are 2 independent parts, one for each index of `grp`. A program takes and returns all parts, laid end to end along the dimension named above; an argument that names none is the same for every part. Nothing has to cross between parts.
Inputs may be any that keep to these rules, and one draw needn't show every extreme that they name: `page_table`: every entry of a layer's table is distinct and every one of the 1024 values occurs once. For each layer, head and micro-batch the 16 blocks form a run; in each run half of the devices receive exactly 8 pages and the others none, so each device receives exactly 256 pages of a layer.
All inputs are finite; a program needn't handle non-finite values.
Results may differ from a plain program's by a relative error of at most 0.017.
Values may be sent and summed in bfloat16 or wider, within the bound.
A program may use at most 128 MiB of HBM per device.

v0:
```python
import math
import jax
import jax.numpy as jnp
from jax import lax
from jax.sharding import PartitionSpec as P

MODEL_WIDTH = 8192
HEAD_SIZE = 128
KEY_VALUE_HEADS = 8
MB_TOK = 64
MICRO_BATCHES = 8
PAGE_TOKENS = 4
eps_norm = 1e-05


def partner_2(x, axis, apart):
    return lax.ppermute(x, axis, [(i, i ^ 1 << apart) for i in range(lax.axis_size(axis))])


def shifted(x, axis, by):
    peers = lax.axis_size(axis)
    pairs = [(i, i + by) for i in range(peers) if 0 <= i + by < peers]
    return lax.ppermute(x, axis, pairs)


def from_root(x, axis, root):
    mine = lax.axis_index(axis) == root
    return lax.psum(jnp.where(mine, x, jnp.zeros_like(x)), axis)


def send_pages(kv_own, page_rows, micro_idx, is_live, kv_cache, first_head, tensor_parallel_width):
    row_count = kv_own.shape[0]
    kv_cols = kv_own.shape[1]
    head_width = kv_cache.shape[2]
    cache_page_count = kv_cache.shape[0]
    held_heads = max(1, kv_cols // head_width)
    unit_cols = kv_cols // held_heads
    blocks = row_count // PAGE_TOKENS
    paged_rows = (
        kv_own.reshape(blocks, PAGE_TOKENS, held_heads, unit_cols)
        .transpose(2, 0, 1, 3)
        .reshape(held_heads * blocks, PAGE_TOKENS * unit_cols)
    )
    target_pages = lax.dynamic_slice(
        page_rows, (first_head, micro_idx * blocks), (held_heads, blocks)
    ).reshape(-1)
    device = target_pages // cache_page_count
    cache_page_index = target_pages % cache_page_count
    page_count = held_heads * blocks
    capacity = 2 * page_count // tensor_parallel_width
    onehot = (
        device[:, None] == jnp.arange(tensor_parallel_width, dtype=jnp.int32)[None, :]
    ).astype(jnp.int32)
    earlier = jnp.cumsum(onehot, axis=0) - onehot
    arrival = jnp.sum(earlier * onehot, axis=1)
    position = device * capacity + arrival
    outgoing = (
        jnp.zeros((tensor_parallel_width * capacity, PAGE_TOKENS * unit_cols), jnp.bfloat16)
        .at[position]
        .set(paged_rows)
    )
    labels = (
        jnp.full((tensor_parallel_width * capacity,), cache_page_count, jnp.int32)
        .at[position]
        .set(jnp.where(is_live, cache_page_index, cache_page_count))
    )
    incoming, landing = (
        lax.all_to_all(outgoing, "tp", split_axis=0, concat_axis=0, tiled=True),
        lax.all_to_all(labels, "tp", split_axis=0, concat_axis=0, tiled=True),
    )
    offsets = jnp.arange(tensor_parallel_width, dtype=jnp.int32) * kv_cols % head_width
    lane_ids = jnp.arange(head_width, dtype=jnp.int32)
    within = jnp.arange(unit_cols, dtype=jnp.int32)
    placer = (lane_ids[None, None, :] == offsets[:, None, None] + within[None, :, None]).astype(
        jnp.bfloat16
    )
    spread = jnp.einsum(
        "snw,swv->snv",
        incoming.reshape(tensor_parallel_width, capacity * PAGE_TOKENS, unit_cols),
        placer,
        preferred_element_type=jnp.float32,
    ).astype(jnp.bfloat16)
    return kv_cache.at[landing].add(
        spread.reshape(tensor_parallel_width * capacity, PAGE_TOKENS, head_width), mode="drop"
    )


def body(tokens, gain, q_weight, kv_weight, out_weight, page_table, segment_ids):
    tensor_parallel_width = lax.axis_size("tp")
    pp_size = lax.axis_size("pp")
    tp_rank = lax.axis_index("tp")
    section_idx = lax.axis_index("pp")
    w_query = q_weight[0]
    w_keyval = kv_weight[0]
    w_output = out_weight[0]
    page_rows = page_table[0]
    local_width = tokens.shape[1]
    row_total = tokens.shape[0]
    row_count = MB_TOK
    head_dim = HEAD_SIZE
    kv_cols = w_keyval.shape[1]
    held_heads = max(1, kv_cols // (2 * head_dim))
    q_heads = w_query.shape[1] // head_dim
    per_kv = q_heads // held_heads
    first_head = tp_rank * kv_cols // (2 * head_dim)
    cache_page_count = KEY_VALUE_HEADS * (row_total // PAGE_TOKENS) // tensor_parallel_width
    score_scale = 1.0 / math.sqrt(head_dim)
    step_count = MICRO_BATCHES + pp_size - 1
    key_pos = jnp.arange(row_total, dtype=jnp.int32)

    def add_columns(block_cols):
        return (
            jnp.dot(block_cols, w_query, preferred_element_type=jnp.float32),
            jnp.dot(block_cols, w_keyval, preferred_element_type=jnp.float32),
        )

    def add_outputs(block_cols):
        return jnp.dot(block_cols, w_output, preferred_element_type=jnp.float32)

    def one_step(step_idx, state_tuple):
        received, kv_buffer, kv_cache, collected = state_tuple
        micro_raw = step_idx - section_idx
        is_live = (micro_raw >= 0) & (micro_raw < MICRO_BATCHES)
        micro_idx = jnp.clip(micro_raw, 0, MICRO_BATCHES - 1)
        row_start = micro_idx * row_count
        first_rows = lax.dynamic_slice_in_dim(tokens, row_start, row_count, 0)
        current = jnp.where(section_idx == 0, first_rows, received)
        widened = current.astype(jnp.float32)
        partial_sq = jnp.sum(widened * widened, axis=1, keepdims=True)
        mean_sq = lax.psum(partial_sq, "tp") / MODEL_WIDTH
        normed = (widened * lax.rsqrt(mean_sq + eps_norm) * gain.astype(jnp.float32)).astype(
            jnp.bfloat16
        )
        query_sum, keyval_sum = add_columns(lax.all_gather(normed, "tp", axis=1, tiled=True))
        query_matrix = query_sum.astype(jnp.bfloat16)
        kv_own = keyval_sum.astype(jnp.bfloat16)
        if tensor_parallel_width > KEY_VALUE_HEADS:
            partner = partner_2(kv_own, "tp", 0)
            first_half = tp_rank % 2 == 0
            head_pair = jnp.where(
                first_half,
                jnp.concatenate([kv_own, partner], axis=1),
                jnp.concatenate([partner, kv_own], axis=1),
            )
        else:
            head_pair = kv_own
        kv_cache = send_pages(
            kv_own, page_rows, micro_idx, is_live, kv_cache, first_head, tensor_parallel_width
        )
        refreshed = lax.dynamic_update_slice_in_dim(kv_buffer, head_pair, row_start, 0)
        kv_buffer = jnp.where(is_live, refreshed, kv_buffer)
        kv_view = kv_buffer.reshape(row_total, held_heads, 2, head_dim)
        grouped_queries = query_matrix.reshape(row_count, held_heads, per_kv, head_dim)
        scores = (
            jnp.einsum(
                "qgpd,kgd->gpqk",
                grouped_queries,
                kv_view[:, :, 0],
                preferred_element_type=jnp.float32,
            )
            * score_scale
        )
        query_pos = row_start + jnp.arange(row_count, dtype=jnp.int32)
        seg_query = lax.dynamic_slice_in_dim(segment_ids, row_start, row_count, 0)
        allowed = (key_pos[None, :] <= query_pos[:, None]) & (
            segment_ids[None, :] == seg_query[:, None]
        )
        scores = jnp.where(allowed[None, None], scores, -1e30)
        row_max = jnp.max(scores, axis=-1, keepdims=True)
        raised = jnp.exp(scores - row_max)
        weights = (raised / jnp.sum(raised, axis=-1, keepdims=True)).astype(jnp.bfloat16)
        attended = jnp.einsum(
            "gpqk,kgd->qgpd", weights, kv_view[:, :, 1], preferred_element_type=jnp.float32
        )
        attended = attended.astype(jnp.bfloat16).reshape(row_count, q_heads * head_dim)
        projected = add_outputs(lax.all_gather(attended, "tp", axis=1, tiled=True))
        produced = (widened + projected).astype(jnp.bfloat16)
        placed = lax.dynamic_update_slice_in_dim(collected, produced, row_start, 0)
        collected = jnp.where(is_live & (section_idx == pp_size - 1), placed, collected)
        handed = shifted(produced, "pp", 1)
        return (handed, kv_buffer, kv_cache, collected)

    initial = (
        jnp.zeros((row_count, local_width), jnp.bfloat16),
        jnp.zeros((row_total, held_heads * 2 * head_dim), jnp.bfloat16),
        jnp.zeros((cache_page_count, PAGE_TOKENS, 2 * head_dim), jnp.bfloat16),
        jnp.zeros((row_total, local_width), jnp.bfloat16),
    )
    finished = lax.fori_loop(0, step_count, one_step, initial)
    whole_final = from_root(finished[3], "pp", pp_size - 1)
    share_rows = row_total // pp_size
    hidden = lax.dynamic_slice_in_dim(whole_final, section_idx * share_rows, share_rows, 0)
    return (hidden, finished[2][None])


def solution(mesh):
    placed = (
        P("grp", "tp"),
        P("pp", "tp"),
        P("pp", None, "tp"),
        P("pp", None, "tp"),
        P("pp", None, "tp"),
        P("pp", None, None),
        P("grp"),
    )
    return jax.shard_map(
        body,
        mesh=mesh,
        in_specs=placed,
        out_specs=(P(("grp", "pp"), "tp"), P("pp", ("grp", "tp"), None, None)),
        check_vma=False,
    )
```

profile of v0, /device:TPU:0, one launch (start us, length us, event | category | flops | bytes accessed | tf_op | source)
XLA Modules:
  0.0 928.2 jit_solution(15119671289388943089)
XLA Ops:
  9.8 821.5 %while.22 = (s32[]{:T(128)}, bf16[64,2048]{1,0:T(8,128)(2,1)S(1)}, bf16[512,512]{1,0:T(8,128)(2,1)S(1)}, bf16[256,4,256]{2,1,0:T(4,128)(2,1)S(1)}, bf16[512,2048...) while((s32[]{:T(128)}, bf16[64,2048]{1,0:T(8,128)(2,1)S(1)}, ...), condition=%wide.region_10.11_spmd.clone, body=%wide.region_0.10_spmd.clone.sunk | while | flops 2923866880 | bytes 66799608 | solution.py:189
  11.1 8.4 psum.24
  31.1 6.4 all-gather.2.cloned.1.call-done
  37.5 5.3 dynamic-slice_select_fusion.4
  43.0 8.8 convolution_convert_fusion.6
  54.5 7.2 all_gather.25
  61.6 9.6 %select_dynamic-update-slice_fusion.2 = (bf16[512,2048]{1,0:T(8,128)(2,1)}, bf16[64,2048]{1,0:T(8,128)(2,1)S(1)}) fusion(bf16[512,2048]{1,0:T(8,128)(2,1)} %get-tuple-element.624, s32[]{:T(128)S(6)} %select_n.328, pred[]{:T(512)S(6)} %and.146, bf16[64,4096]{1,0:T(8,128)(2,1)S(1)} %all_gather.25, bf16[4096,2048]{1,0:T(8,128)(2,1)} %get-tuple-element.658, ...), kind=kOutput, calls=%fused_computation.27.clone.1 | convolution fusion | flops 1074266112 | bytes 18350084 | tf_op jit(solution)/shard_map/while/body/eval_jaxpr/dot_general | solution.py:118
  88.7 5.8 psum.24
  106.2 5.6 all-gather.2.cloned.1.call-done
  111.8 5.3 dynamic-slice_select_fusion.4
  117.3 8.8 convolution_convert_fusion.6
  129.2 7.2 all_gather.25
  136.3 9.5 %select_dynamic-update-slice_fusion.2 = (bf16[512,2048]{1,0:T(8,128)(2,1)}, bf16[64,2048]{1,0:T(8,128)(2,1)S(1)}) fusion(bf16[512,2048]{1,0:T(8,128)(2,1)} %get-tuple-element.624, s32[]{:T(128)S(6)} %select_n.328, pred[]{:T(512)S(6)} %and.146, bf16[64,4096]{1,0:T(8,128)(2,1)S(1)} %all_gather.25, bf16[4096,2048]{1,0:T(8,128)(2,1)} %get-tuple-element.658, ...), kind=kOutput, calls=%fused_computation.27.clone.1 | convolution fusion | flops 1074266112 | bytes 18350084 | tf_op jit(solution)/shard_map/while/body/eval_jaxpr/dot_general | solution.py:118
  163.0 5.8 psum.24
  180.5 5.6 all-gather.2.cloned.1.call-done
  186.1 5.3 dynamic-slice_select_fusion.4
  191.6 8.8 convolution_convert_fusion.6
  203.0 7.2 all_gather.25
  210.2 9.5 %select_dynamic-update-slice_fusion.2 = (bf16[512,2048]{1,0:T(8,128)(2,1)}, bf16[64,2048]{1,0:T(8,128)(2,1)S(1)}) fusion(bf16[512,2048]{1,0:T(8,128)(2,1)} %get-tuple-element.624, s32[]{:T(128)S(6)} %select_n.328, pred[]{:T(512)S(6)} %and.146, bf16[64,4096]{1,0:T(8,128)(2,1)S(1)} %all_gather.25, bf16[4096,2048]{1,0:T(8,128)(2,1)} %get-tuple-element.658, ...), kind=kOutput, calls=%fused_computation.27.clone.1 | convolution fusion | flops 1074266112 | bytes 18350084 | tf_op jit(solution)/shard_map/while/body/eval_jaxpr/dot_general | solution.py:118
  237.7 5.8 psum.24
  260.3 5.3 dynamic-slice_select_fusion.4
  265.8 8.8 convolution_convert_fusion.6
  277.6 7.2 all_gather.25
  284.8 9.5 %select_dynamic-update-slice_fusion.2 = (bf16[512,2048]{1,0:T(8,128)(2,1)}, bf16[64,2048]{1,0:T(8,128)(2,1)S(1)}) fusion(bf16[512,2048]{1,0:T(8,128)(2,1)} %get-tuple-element.624, s32[]{:T(128)S(6)} %select_n.328, pred[]{:T(512)S(6)} %and.146, bf16[64,4096]{1,0:T(8,128)(2,1)S(1)} %all_gather.25, bf16[4096,2048]{1,0:T(8,128)(2,1)} %get-tuple-element.658, ...), kind=kOutput, calls=%fused_computation.27.clone.1 | convolution fusion | flops 1074266112 | bytes 18350084 | tf_op jit(solution)/shard_map/while/body/eval_jaxpr/dot_general | solution.py:118
  311.4 5.8 psum.24
  328.9 5.6 all-gather.2.cloned.1.call-done
  334.5 5.3 dynamic-slice_select_fusion.4
  340.0 8.8 convolution_convert_fusion.6
  351.5 7.2 all_gather.25
  358.6 9.5 %select_dynamic-update-slice_fusion.2 = (bf16[512,2048]{1,0:T(8,128)(2,1)}, bf16[64,2048]{1,0:T(8,128)(2,1)S(1)}) fusion(bf16[512,2048]{1,0:T(8,128)(2,1)} %get-tuple-element.624, s32[]{:T(128)S(6)} %select_n.328, pred[]{:T(512)S(6)} %and.146, bf16[64,4096]{1,0:T(8,128)(2,1)S(1)} %all_gather.25, bf16[4096,2048]{1,0:T(8,128)(2,1)} %get-tuple-element.658, ...), kind=kOutput, calls=%fused_computation.27.clone.1 | convolution fusion | flops 1074266112 | bytes 18350084 | tf_op jit(solution)/shard_map/while/body/eval_jaxpr/dot_general | solution.py:118
  386.1 5.8 psum.24
  403.6 5.6 all-gather.2.cloned.1.call-done
  409.2 5.3 dynamic-slice_select_fusion.4
  414.7 8.8 convolution_convert_fusion.6
  426.5 7.2 all_gather.25
  433.7 9.5 %select_dynamic-update-slice_fusion.2 = (bf16[512,2048]{1,0:T(8,128)(2,1)}, bf16[64,2048]{1,0:T(8,128)(2,1)S(1)}) fusion(bf16[512,2048]{1,0:T(8,128)(2,1)} %get-tuple-element.624, s32[]{:T(128)S(6)} %select_n.328, pred[]{:T(512)S(6)} %and.146, bf16[64,4096]{1,0:T(8,128)(2,1)S(1)} %all_gather.25, bf16[4096,2048]{1,0:T(8,128)(2,1)} %get-tuple-element.658, ...), kind=kOutput, calls=%fused_computation.27.clone.1 | convolution fusion | flops 1074266112 | bytes 18350084 | tf_op jit(solution)/shard_map/while/body/eval_jaxpr/dot_general | solution.py:118
  460.4 5.8 psum.24
  477.8 5.6 all-gather.2.cloned.1.call-done
  488.9 8.8 convolution_convert_fusion.6
  500.2 7.2 all_gather.25
  507.4 9.5 %select_dynamic-update-slice_fusion.2 = (bf16[512,2048]{1,0:T(8,128)(2,1)}, bf16[64,2048]{1,0:T(8,128)(2,1)S(1)}) fusion(bf16[512,2048]{1,0:T(8,128)(2,1)} %get-tuple-element.624, s32[]{:T(128)S(6)} %select_n.328, pred[]{:T(512)S(6)} %and.146, bf16[64,4096]{1,0:T(8,128)(2,1)S(1)} %all_gather.25, bf16[4096,2048]{1,0:T(8,128)(2,1)} %get-tuple-element.658, ...), kind=kOutput, calls=%fused_computation.27.clone.1 | convolution fusion | flops 1074266112 | bytes 18350084 | tf_op jit(solution)/shard_map/while/body/eval_jaxpr/dot_general | solution.py:118
  535.0 5.8 psum.24
  552.5 5.5 all-gather.2.cloned.1.call-done
  558.0 5.3 dynamic-slice_select_fusion.4
  563.5 8.8 convolution_convert_fusion.6
  575.3 7.2 all_gather.25
  582.4 9.5 %select_dynamic-update-slice_fusion.2 = (bf16[512,2048]{1,0:T(8,128)(2,1)}, bf16[64,2048]{1,0:T(8,128)(2,1)S(1)}) fusion(bf16[512,2048]{1,0:T(8,128)(2,1)} %get-tuple-element.624, s32[]{:T(128)S(6)} %select_n.328, pred[]{:T(512)S(6)} %and.146, bf16[64,4096]{1,0:T(8,128)(2,1)S(1)} %all_gather.25, bf16[4096,2048]{1,0:T(8,128)(2,1)} %get-tuple-element.658, ...), kind=kOutput, calls=%fused_computation.27.clone.1 | convolution fusion | flops 1074266112 | bytes 18350084 | tf_op jit(solution)/shard_map/while/body/eval_jaxpr/dot_general | solution.py:118
  609.1 5.8 psum.24
  626.5 5.7 all-gather.2.cloned.1.call-done
  632.2 5.3 dynamic-slice_select_fusion.4
  637.7 8.8 convolution_convert_fusion.6
  649.5 7.2 all_gather.25
  656.6 9.5 %select_dynamic-update-slice_fusion.2 = (bf16[512,2048]{1,0:T(8,128)(2,1)}, bf16[64,2048]{1,0:T(8,128)(2,1)S(1)}) fusion(bf16[512,2048]{1,0:T(8,128)(2,1)} %get-tuple-element.624, s32[]{:T(128)S(6)} %select_n.328, pred[]{:T(512)S(6)} %and.146, bf16[64,4096]{1,0:T(8,128)(2,1)S(1)} %all_gather.25, bf16[4096,2048]{1,0:T(8,128)(2,1)} %get-tuple-element.658, ...), kind=kOutput, calls=%fused_computation.27.clone.1 | convolution fusion | flops 1074266112 | bytes 18350084 | tf_op jit(solution)/shard_map/while/body/eval_jaxpr/dot_general | solution.py:118
  683.8 5.8 psum.24
  701.3 5.5 all-gather.2.cloned.1.call-done
  706.8 5.3 dynamic-slice_select_fusion.4
  712.3 8.8 convolution_convert_fusion.6
  724.1 7.2 all_gather.25
  731.2 9.5 %select_dynamic-update-slice_fusion.2 = (bf16[512,2048]{1,0:T(8,128)(2,1)}, bf16[64,2048]{1,0:T(8,128)(2,1)S(1)}) fusion(bf16[512,2048]{1,0:T(8,128)(2,1)} %get-tuple-element.624, s32[]{:T(128)S(6)} %select_n.328, pred[]{:T(512)S(6)} %and.146, bf16[64,4096]{1,0:T(8,128)(2,1)S(1)} %all_gather.25, bf16[4096,2048]{1,0:T(8,128)(2,1)} %get-tuple-element.658, ...), kind=kOutput, calls=%fused_computation.27.clone.1 | convolution fusion | flops 1074266112 | bytes 18350084 | tf_op jit(solution)/shard_map/while/body/eval_jaxpr/dot_general | solution.py:118
  758.4 5.8 psum.24
  786.4 8.8 convolution_convert_fusion.6
  798.2 7.2 all_gather.25
  805.4 9.5 %select_dynamic-update-slice_fusion.2 = (bf16[512,2048]{1,0:T(8,128)(2,1)}, bf16[64,2048]{1,0:T(8,128)(2,1)S(1)}) fusion(bf16[512,2048]{1,0:T(8,128)(2,1)} %get-tuple-element.624, s32[]{:T(128)S(6)} %select_n.328, pred[]{:T(512)S(6)} %and.146, bf16[64,4096]{1,0:T(8,128)(2,1)S(1)} %all_gather.25, bf16[4096,2048]{1,0:T(8,128)(2,1)} %get-tuple-element.658, ...), kind=kOutput, calls=%fused_computation.27.clone.1 | convolution fusion | flops 1074266112 | bytes 18350084 | tf_op jit(solution)/shard_map/while/body/eval_jaxpr/dot_general | solution.py:118
  832.9 86.3 %all-reduce.2.cloned.1.call-done = bf16[512,2048]{1,0:T(8,128)(2,1)} async-done(((bf16[512,2048]{1,0:T(8,128)(2,1)}), bf16[512,2048]{1,0:T(8,128)(2,1)}) %all-reduce.2.cloned.1.call-update) | async-done | bytes 2097168 | tf_op jit(solution)/shard_map/psum | solution.py:28
  (579 shorter events, 378.1 us)
Async XLA Ops:
  8.0 1.8 copy-start.2
  8.0 1.8 copy-start.3
  9.8 27.7 %all-gather.2.cloned.1.call-start = ((), (), s32[]{:S(2)}) async-start(), calls=%async_computation.3 | async-start | bytes 1310720 | tf_op jit(solution)/shard_map/while/body/eval_jaxpr/all_gather | solution.py:134
  23.0 6.9 all-to-all-start
  37.5 5.5 copy-start
  71.2 16.3 %collective-permute-start = (bf16[64,2048]{1,0:T(8,128)(2,1)S(1)}, bf16[64,2048]{1,0:T(8,128)(2,1)S(1)}, u32[]{:S(2)}, u32[]{:S(2)}) collective-permute-start(bf16[64,2048]{1,0:T(8,128)(2,1)S(1)} %get-tuple-element.589), channel_id=1, source_target_pairs={{0,1},{1,2},{2,3},{4,5},{5,6},{6,7},{8,9},{9,10},{10,11},{12,13},{... | collective-permute-start | bytes 786440 | tf_op jit(solution)/shard_map/while/body/eval_jaxpr/ppermute | solution.py:23
  76.0 7.9 all-to-all-start.1
  87.5 24.3 %all-gather.2.cloned.1.call-start = ((), (), s32[]{:S(2)}) async-start(), calls=%async_computation.3 | async-start | bytes 1310720 | tf_op jit(solution)/shard_map/while/body/eval_jaxpr/all_gather | solution.py:134
  98.0 6.9 all-to-all-start
  111.8 5.5 copy-start
  145.9 15.9 %collective-permute-start = (bf16[64,2048]{1,0:T(8,128)(2,1)S(1)}, bf16[64,2048]{1,0:T(8,128)(2,1)S(1)}, u32[]{:S(2)}, u32[]{:S(2)}) collective-permute-start(bf16[64,2048]{1,0:T(8,128)(2,1)S(1)} %get-tuple-element.589), channel_id=1, source_target_pairs={{0,1},{1,2},{2,3},{4,5},{5,6},{6,7},{8,9},{9,10},{10,11},{12,13},{... | collective-permute-start | bytes 786440 | tf_op jit(solution)/shard_map/while/body/eval_jaxpr/ppermute | solution.py:23
  150.3 7.9 all-to-all-start.1
  161.8 24.3 %all-gather.2.cloned.1.call-start = ((), (), s32[]{:S(2)}) async-start(), calls=%async_computation.3 | async-start | bytes 1310720 | tf_op jit(solution)/shard_map/while/body/eval_jaxpr/all_gather | solution.py:134
  172.3 6.9 all-to-all-start
  186.1 5.5 copy-start
  219.7 16.7 %collective-permute-start = (bf16[64,2048]{1,0:T(8,128)(2,1)S(1)}, bf16[64,2048]{1,0:T(8,128)(2,1)S(1)}, u32[]{:S(2)}, u32[]{:S(2)}) collective-permute-start(bf16[64,2048]{1,0:T(8,128)(2,1)S(1)} %get-tuple-element.589), channel_id=1, source_target_pairs={{0,1},{1,2},{2,3},{4,5},{5,6},{6,7},{8,9},{9,10},{10,11},{12,13},{... | collective-permute-start | bytes 786440 | tf_op jit(solution)/shard_map/while/body/eval_jaxpr/ppermute | solution.py:23
  225.0 7.9 all-to-all-start.1
  236.5 23.8 %all-gather.2.cloned.1.call-start = ((), (), s32[]{:S(2)}) async-start(), calls=%async_computation.3 | async-start | bytes 1310720 | tf_op jit(solution)/shard_map/while/body/eval_jaxpr/all_gather | solution.py:134
  247.0 6.9 all-to-all-start
  260.3 5.5 copy-start
  294.3 15.9 %collective-permute-start = (bf16[64,2048]{1,0:T(8,128)(2,1)S(1)}, bf16[64,2048]{1,0:T(8,128)(2,1)S(1)}, u32[]{:S(2)}, u32[]{:S(2)}) collective-permute-start(bf16[64,2048]{1,0:T(8,128)(2,1)S(1)} %get-tuple-element.589), channel_id=1, source_target_pairs={{0,1},{1,2},{2,3},{4,5},{5,6},{6,7},{8,9},{9,10},{10,11},{12,13},{... | collective-permute-start | bytes 786440 | tf_op jit(solution)/shard_map/while/body/eval_jaxpr/ppermute | solution.py:23
  298.8 7.9 all-to-all-start.1
  310.2 24.3 %all-gather.2.cloned.1.call-start = ((), (), s32[]{:S(2)}) async-start(), calls=%async_computation.3 | async-start | bytes 1310720 | tf_op jit(solution)/shard_map/while/body/eval_jaxpr/all_gather | solution.py:134
  320.7 6.9 all-to-all-start
  334.5 5.5 copy-start
  368.2 16.7 %collective-permute-start = (bf16[64,2048]{1,0:T(8,128)(2,1)S(1)}, bf16[64,2048]{1,0:T(8,128)(2,1)S(1)}, u32[]{:S(2)}, u32[]{:S(2)}) collective-permute-start(bf16[64,2048]{1,0:T(8,128)(2,1)S(1)} %get-tuple-element.589), channel_id=1, source_target_pairs={{0,1},{1,2},{2,3},{4,5},{5,6},{6,7},{8,9},{9,10},{10,11},{12,13},{... | collective-permute-start | bytes 786440 | tf_op jit(solution)/shard_map/while/body/eval_jaxpr/ppermute | solution.py:23
  373.4 7.9 all-to-all-start.1
  384.9 24.3 %all-gather.2.cloned.1.call-start = ((), (), s32[]{:S(2)}) async-start(), calls=%async_computation.3 | async-start | bytes 1310720 | tf_op jit(solution)/shard_map/while/body/eval_jaxpr/all_gather | solution.py:134
  395.4 6.9 all-to-all-start
  409.2 5.5 copy-start
  443.2 15.9 %collective-permute-start = (bf16[64,2048]{1,0:T(8,128)(2,1)S(1)}, bf16[64,2048]{1,0:T(8,128)(2,1)S(1)}, u32[]{:S(2)}, u32[]{:S(2)}) collective-permute-start(bf16[64,2048]{1,0:T(8,128)(2,1)S(1)} %get-tuple-element.589), channel_id=1, source_target_pairs={{0,1},{1,2},{2,3},{4,5},{5,6},{6,7},{8,9},{9,10},{10,11},{12,13},{... | collective-permute-start | bytes 786440 | tf_op jit(solution)/shard_map/while/body/eval_jaxpr/ppermute | solution.py:23
  447.7 7.9 all-to-all-start.1
  459.1 24.2 %all-gather.2.cloned.1.call-start = ((), (), s32[]{:S(2)}) async-start(), calls=%async_computation.3 | async-start | bytes 1310720 | tf_op jit(solution)/shard_map/while/body/eval_jaxpr/all_gather | solution.py:134
  469.6 6.9 all-to-all-start
  483.4 5.5 copy-start
  516.9 16.8 %collective-permute-start = (bf16[64,2048]{1,0:T(8,128)(2,1)S(1)}, bf16[64,2048]{1,0:T(8,128)(2,1)S(1)}, u32[]{:S(2)}, u32[]{:S(2)}) collective-permute-start(bf16[64,2048]{1,0:T(8,128)(2,1)S(1)} %get-tuple-element.589), channel_id=1, source_target_pairs={{0,1},{1,2},{2,3},{4,5},{5,6},{6,7},{8,9},{9,10},{10,11},{12,13},{... | collective-permute-start | bytes 786440 | tf_op jit(solution)/shard_map/while/body/eval_jaxpr/ppermute | solution.py:23
  522.3 7.9 all-to-all-start.1
  533.7 24.2 %all-gather.2.cloned.1.call-start = ((), (), s32[]{:S(2)}) async-start(), calls=%async_computation.3 | async-start | bytes 1310720 | tf_op jit(solution)/shard_map/while/body/eval_jaxpr/all_gather | solution.py:134
  544.3 6.9 all-to-all-start
  558.0 5.5 copy-start
  592.0 15.9 %collective-permute-start = (bf16[64,2048]{1,0:T(8,128)(2,1)S(1)}, bf16[64,2048]{1,0:T(8,128)(2,1)S(1)}, u32[]{:S(2)}, u32[]{:S(2)}) collective-permute-start(bf16[64,2048]{1,0:T(8,128)(2,1)S(1)} %get-tuple-element.589), channel_id=1, source_target_pairs={{0,1},{1,2},{2,3},{4,5},{5,6},{6,7},{8,9},{9,10},{10,11},{12,13},{... | collective-permute-start | bytes 786440 | tf_op jit(solution)/shard_map/while/body/eval_jaxpr/ppermute | solution.py:23
  596.4 7.9 all-to-all-start.1
  607.9 24.3 %all-gather.2.cloned.1.call-start = ((), (), s32[]{:S(2)}) async-start(), calls=%async_computation.3 | async-start | bytes 1310720 | tf_op jit(solution)/shard_map/while/body/eval_jaxpr/all_gather | solution.py:134
  618.4 6.9 all-to-all-start
  632.2 5.5 copy-start
  666.2 16.4 %collective-permute-start = (bf16[64,2048]{1,0:T(8,128)(2,1)S(1)}, bf16[64,2048]{1,0:T(8,128)(2,1)S(1)}, u32[]{:S(2)}, u32[]{:S(2)}) collective-permute-start(bf16[64,2048]{1,0:T(8,128)(2,1)S(1)} %get-tuple-element.589), channel_id=1, source_target_pairs={{0,1},{1,2},{2,3},{4,5},{5,6},{6,7},{8,9},{9,10},{10,11},{12,13},{... | collective-permute-start | bytes 786440 | tf_op jit(solution)/shard_map/while/body/eval_jaxpr/ppermute | solution.py:23
  671.0 7.9 all-to-all-start.1
  682.6 24.2 %all-gather.2.cloned.1.call-start = ((), (), s32[]{:S(2)}) async-start(), calls=%async_computation.3 | async-start | bytes 1310720 | tf_op jit(solution)/shard_map/while/body/eval_jaxpr/all_gather | solution.py:134
  693.1 6.9 all-to-all-start
  706.8 5.5 copy-start
  740.8 16.4 %collective-permute-start = (bf16[64,2048]{1,0:T(8,128)(2,1)S(1)}, bf16[64,2048]{1,0:T(8,128)(2,1)S(1)}, u32[]{:S(2)}, u32[]{:S(2)}) collective-permute-start(bf16[64,2048]{1,0:T(8,128)(2,1)S(1)} %get-tuple-element.589), channel_id=1, source_target_pairs={{0,1},{1,2},{2,3},{4,5},{5,6},{6,7},{8,9},{9,10},{10,11},{12,13},{... | collective-permute-start | bytes 786440 | tf_op jit(solution)/shard_map/while/body/eval_jaxpr/ppermute | solution.py:23
  745.6 7.9 all-to-all-start.1
  757.2 23.8 %all-gather.2.cloned.1.call-start = ((), (), s32[]{:S(2)}) async-start(), calls=%async_computation.3 | async-start | bytes 1310720 | tf_op jit(solution)/shard_map/while/body/eval_jaxpr/all_gather | solution.py:134
  767.7 6.9 all-to-all-start
  780.9 5.5 copy-start
  814.9 16.4 %collective-permute-start = (bf16[64,2048]{1,0:T(8,128)(2,1)S(1)}, bf16[64,2048]{1,0:T(8,128)(2,1)S(1)}, u32[]{:S(2)}, u32[]{:S(2)}) collective-permute-start(bf16[64,2048]{1,0:T(8,128)(2,1)S(1)} %get-tuple-element.589), channel_id=1, source_target_pairs={{0,1},{1,2},{2,3},{4,5},{5,6},{6,7},{8,9},{9,10},{10,11},{12,13},{... | collective-permute-start | bytes 786440 | tf_op jit(solution)/shard_map/while/body/eval_jaxpr/ppermute | solution.py:23
  819.8 7.9 all-to-all-start.1
  831.3 1.6 copy-start.1
  831.3 87.9 %all-reduce.2.cloned.1.call-start = ((), (), s32[]{:S(2)}) async-start(), calls=%async_computation.2 | async-start | bytes 4194304 | tf_op jit(solution)/shard_map/psum | solution.py:28
Sparse Core Ops, SparseCore 0:
  20.5 17.0 all-gather.1
  95.5 16.2 all-gather.1
  169.8 16.2 all-gather.1
  244.5 15.7 all-gather.1
  318.2 16.2 all-gather.1
  392.9 16.2 all-gather.1
  467.1 16.2 all-gather.1
  541.8 16.1 all-gather.1
  615.9 16.3 all-gather.1
  690.6 16.1 all-gather.1
  765.1 15.7 all-gather.1
Sparse Core Ops, SparseCore 1:
  834.2 85.0 all-reduce.1
where the time goes:
time: 932 us; the launch traced here: 928 us
  matrix products  285 us (31%)
  waiting for transfers between devices  231 us (25%)
  blocking collectives  145 us (16%)
  starting transfers between devices  110 us (12%)
  other arithmetic  70.3 us (8%)
  local copies, waits for them, and re-layouts  69.7 us (7%)
  between operations  15.2 us (2%)
    dot_general x11, matrix products, add_outputs(): return jnp.dot(block_cols, w_output, preferred_element_type=jnp.float32)  105 us
    dot_general x11, matrix products, add_columns(): jnp.dot(block_cols, w_query, preferred_element_type=jnp.float32)  96.7 us
    psum x1, waiting for transfers between devices, from_root(): return lax.psum(jnp.where(mine, x, jnp.zeros_like(x)), axis)  86.3 us
    all_gather x11, blocking collectives, one_step(): projected = add_outputs(lax.all_gather(attended, 'tp', axis=1, tiled=True))  78.7 us
    psum x11, blocking collectives, one_step(): mean_sq = lax.psum(partial_sq, 'tp') / MODEL_WIDTH  66.2 us
    all_gather x11, waiting for transfers between devices, one_step(): lax.all_gather(normed, 'tp', axis=1, tiled=True)  61.4 us
    dot_general x11, matrix products, add_columns(): jnp.dot(block_cols, w_keyval, preferred_element_type=jnp.float32)  58.8 us
    all_to_all x11, waiting for transfers between devices, send_pages(): lax.all_to_all(outgoing, 'tp', split_axis=0, concat_axis=0, tiled=True)  47.7 us
  transfers between devices with their start and end apart: 45, of which 34 were waited for; matrix products, arithmetic and copies ran while one was open for 10% of the time, Pallas kernels for 0%

commit v1 on v0

--- a/solution.py
+++ b/solution.py
@@ -173,7 +173,7 @@
             "gpqk,kgd->qgpd", weights, kv_view[:, :, 1], preferred_element_type=jnp.float32
         )
         attended = attended.astype(jnp.bfloat16).reshape(row_count, q_heads * head_dim)
-        projected = add_outputs(lax.all_gather(attended, "tp", axis=1, tiled=True))
+        projected = add_outputs(jnp.concatenate(lax.all_gather(attended, "tp"), axis=1))
         produced = (widened + projected).astype(jnp.bfloat16)
         placed = lax.dynamic_update_slice_in_dim(collected, produced, row_start, 0)
         collected = jnp.where(is_live & (section_idx == pp_size - 1), placed, collected)

time: 932 us -> 933 us (level)
  no operation moved by 1% of the time
where the time goes in v1:
time: 933 us; the launch traced here: 929 us
  matrix products  285 us (31%)
  waiting for transfers between devices  231 us (25%)
  blocking collectives  145 us (16%)
  starting transfers between devices  109 us (12%)
  other arithmetic  70.3 us (8%)
  local copies, waits for them, and re-layouts  70.1 us (8%)
  between operations  15.2 us (2%)
    dot_general x11, matrix products, add_outputs(): return jnp.dot(block_cols, w_output, preferred_element_type=jnp.float32)  105 us
    dot_general x11, matrix products, add_columns(): jnp.dot(block_cols, w_query, preferred_element_type=jnp.float32)  96.7 us
    psum x1, waiting for transfers between devices, from_root(): return lax.psum(jnp.where(mine, x, jnp.zeros_like(x)), axis)  86.3 us
    all_gather x11, blocking collectives, one_step(): lax.all_gather(attended, 'tp')  78.7 us
    psum x11, blocking collectives, one_step(): mean_sq = lax.psum(partial_sq, 'tp') / MODEL_WIDTH  66.2 us
    all_gather x11, waiting for transfers between devices, one_step(): lax.all_gather(normed, 'tp', axis=1, tiled=True)  61.4 us
    dot_general x11, matrix products, add_columns(): jnp.dot(block_cols, w_keyval, preferred_element_type=jnp.float32)  58.8 us
    all_to_all x11, waiting for transfers between devices, send_pages(): lax.all_to_all(outgoing, 'tp', split_axis=0, concat_axis=0, tiled=True)  47.7 us
  transfers between devices with their start and end apart: 45, of which 34 were waited for; matrix products, arithmetic and copies ran while one was open for 10% of the time, Pallas kernels for 0%

profile of v1, /device:TPU:0, one launch (start us, length us, event | category | flops | bytes accessed | tf_op | source)
XLA Modules:
  0.0 929.0 jit_solution(18335167146415472211)
XLA Ops:
  9.8 822.2 %while.22 = (s32[]{:T(128)}, bf16[64,2048]{1,0:T(8,128)(2,1)S(1)}, bf16[512,512]{1,0:T(8,128)(2,1)S(1)}, bf16[256,4,256]{2,1,0:T(4,128)(2,1)S(1)}, bf16[512,2048...) while((s32[]{:T(128)}, bf16[64,2048]{1,0:T(8,128)(2,1)S(1)}, ...), condition=%wide.region_10.11_spmd.clone, body=%wide.region_0.10_spmd.clone.sunk | while | flops 2923866880 | bytes 67848184 | solution.py:189
  11.1 8.4 psum.24
  31.1 6.4 all-gather.2.cloned.1.call-done
  37.5 5.3 dynamic-slice_select_fusion.4
  43.0 8.8 convolution_convert_fusion.6
  54.5 7.2 all_gather.25
  61.7 9.6 %select_dynamic-update-slice_fusion.2 = (bf16[512,2048]{1,0:T(8,128)(2,1)}, bf16[64,2048]{1,0:T(8,128)(2,1)S(1)}) fusion(bf16[512,2048]{1,0:T(8,128)(2,1)} %get-tuple-element.624, s32[]{:T(128)S(6)} %select_n.328, pred[]{:T(512)S(6)} %and.146, bf16[64,4096]{1,0:T(8,128)(2,1)S(1)} %bitcast.124, bf16[4096,2048]{1,0:T(8,128)(2,1)} %get-tuple-element.658, ...), kind=kOutput, calls=%fused_computation.27.clone.1 | convolution fusion | flops 1074266112 | bytes 18350084 | tf_op jit(solution)/shard_map/while/body/eval_jaxpr/dot_general | solution.py:118
  88.8 5.8 psum.24
  106.2 5.6 all-gather.2.cloned.1.call-done
  111.9 5.3 dynamic-slice_select_fusion.4
  117.4 8.8 convolution_convert_fusion.6
  129.2 7.2 all_gather.25
  136.4 9.6 %select_dynamic-update-slice_fusion.2 = (bf16[512,2048]{1,0:T(8,128)(2,1)}, bf16[64,2048]{1,0:T(8,128)(2,1)S(1)}) fusion(bf16[512,2048]{1,0:T(8,128)(2,1)} %get-tuple-element.624, s32[]{:T(128)S(6)} %select_n.328, pred[]{:T(512)S(6)} %and.146, bf16[64,4096]{1,0:T(8,128)(2,1)S(1)} %bitcast.124, bf16[4096,2048]{1,0:T(8,128)(2,1)} %get-tuple-element.658, ...), kind=kOutput, calls=%fused_computation.27.clone.1 | convolution fusion | flops 1074266112 | bytes 18350084 | tf_op jit(solution)/shard_map/while/body/eval_jaxpr/dot_general | solution.py:118
  163.2 5.8 psum.24
  180.6 5.6 all-gather.2.cloned.1.call-done
  186.2 5.3 dynamic-slice_select_fusion.4
  191.7 8.8 convolution_convert_fusion.6
  203.2 7.2 all_gather.25
  210.4 9.6 %select_dynamic-update-slice_fusion.2 = (bf16[512,2048]{1,0:T(8,128)(2,1)}, bf16[64,2048]{1,0:T(8,128)(2,1)S(1)}) fusion(bf16[512,2048]{1,0:T(8,128)(2,1)} %get-tuple-element.624, s32[]{:T(128)S(6)} %select_n.328, pred[]{:T(512)S(6)} %and.146, bf16[64,4096]{1,0:T(8,128)(2,1)S(1)} %bitcast.124, bf16[4096,2048]{1,0:T(8,128)(2,1)} %get-tuple-element.658, ...), kind=kOutput, calls=%fused_computation.27.clone.1 | convolution fusion | flops 1074266112 | bytes 18350084 | tf_op jit(solution)/shard_map/while/body/eval_jaxpr/dot_general | solution.py:118
  237.9 5.8 psum.24
  260.5 5.3 dynamic-slice_select_fusion.4
  266.0 8.8 convolution_convert_fusion.6
  277.8 7.2 all_gather.25
  285.0 9.6 %select_dynamic-update-slice_fusion.2 = (bf16[512,2048]{1,0:T(8,128)(2,1)}, bf16[64,2048]{1,0:T(8,128)(2,1)S(1)}) fusion(bf16[512,2048]{1,0:T(8,128)(2,1)} %get-tuple-element.624, s32[]{:T(128)S(6)} %select_n.328, pred[]{:T(512)S(6)} %and.146, bf16[64,4096]{1,0:T(8,128)(2,1)S(1)} %bitcast.124, bf16[4096,2048]{1,0:T(8,128)(2,1)} %get-tuple-element.658, ...), kind=kOutput, calls=%fused_computation.27.clone.1 | convolution fusion | flops 1074266112 | bytes 18350084 | tf_op jit(solution)/shard_map/while/body/eval_jaxpr/dot_general | solution.py:118
  311.7 5.8 psum.24
  329.2 5.6 all-gather.2.cloned.1.call-done
  334.8 5.3 dynamic-slice_select_fusion.4
  340.3 8.8 convolution_convert_fusion.6
  351.8 7.2 all_gather.25
  358.9 9.6 %select_dynamic-update-slice_fusion.2 = (bf16[512,2048]{1,0:T(8,128)(2,1)}, bf16[64,2048]{1,0:T(8,128)(2,1)S(1)}) fusion(bf16[512,2048]{1,0:T(8,128)(2,1)} %get-tuple-element.624, s32[]{:T(128)S(6)} %select_n.328, pred[]{:T(512)S(6)} %and.146, bf16[64,4096]{1,0:T(8,128)(2,1)S(1)} %bitcast.124, bf16[4096,2048]{1,0:T(8,128)(2,1)} %get-tuple-element.658, ...), kind=kOutput, calls=%fused_computation.27.clone.1 | convolution fusion | flops 1074266112 | bytes 18350084 | tf_op jit(solution)/shard_map/while/body/eval_jaxpr/dot_general | solution.py:118
  386.5 5.8 psum.24
  403.9 5.6 all-gather.2.cloned.1.call-done
  409.5 5.3 dynamic-slice_select_fusion.4
  415.0 8.8 convolution_convert_fusion.6
  426.9 7.2 all_gather.25
  434.1 9.6 %select_dynamic-update-slice_fusion.2 = (bf16[512,2048]{1,0:T(8,128)(2,1)}, bf16[64,2048]{1,0:T(8,128)(2,1)S(1)}) fusion(bf16[512,2048]{1,0:T(8,128)(2,1)} %get-tuple-element.624, s32[]{:T(128)S(6)} %select_n.328, pred[]{:T(512)S(6)} %and.146, bf16[64,4096]{1,0:T(8,128)(2,1)S(1)} %bitcast.124, bf16[4096,2048]{1,0:T(8,128)(2,1)} %get-tuple-element.658, ...), kind=kOutput, calls=%fused_computation.27.clone.1 | convolution fusion | flops 1074266112 | bytes 18350084 | tf_op jit(solution)/shard_map/while/body/eval_jaxpr/dot_general | solution.py:118
  460.8 5.8 psum.24
  478.2 5.6 all-gather.2.cloned.1.call-done
  489.3 8.8 convolution_convert_fusion.6
  500.7 7.2 all_gather.25
  507.9 9.6 %select_dynamic-update-slice_fusion.2 = (bf16[512,2048]{1,0:T(8,128)(2,1)}, bf16[64,2048]{1,0:T(8,128)(2,1)S(1)}) fusion(bf16[512,2048]{1,0:T(8,128)(2,1)} %get-tuple-element.624, s32[]{:T(128)S(6)} %select_n.328, pred[]{:T(512)S(6)} %and.146, bf16[64,4096]{1,0:T(8,128)(2,1)S(1)} %bitcast.124, bf16[4096,2048]{1,0:T(8,128)(2,1)} %get-tuple-element.658, ...), kind=kOutput, calls=%fused_computation.27.clone.1 | convolution fusion | flops 1074266112 | bytes 18350084 | tf_op jit(solution)/shard_map/while/body/eval_jaxpr/dot_general | solution.py:118
  535.4 5.8 psum.24
  552.9 5.5 all-gather.2.cloned.1.call-done
  558.5 5.3 dynamic-slice_select_fusion.4
  563.9 8.8 convolution_convert_fusion.6
  575.7 7.2 all_gather.25
  582.9 9.6 %select_dynamic-update-slice_fusion.2 = (bf16[512,2048]{1,0:T(8,128)(2,1)}, bf16[64,2048]{1,0:T(8,128)(2,1)S(1)}) fusion(bf16[512,2048]{1,0:T(8,128)(2,1)} %get-tuple-element.624, s32[]{:T(128)S(6)} %select_n.328, pred[]{:T(512)S(6)} %and.146, bf16[64,4096]{1,0:T(8,128)(2,1)S(1)} %bitcast.124, bf16[4096,2048]{1,0:T(8,128)(2,1)} %get-tuple-element.658, ...), kind=kOutput, calls=%fused_computation.27.clone.1 | convolution fusion | flops 1074266112 | bytes 18350084 | tf_op jit(solution)/shard_map/while/body/eval_jaxpr/dot_general | solution.py:118
  609.6 5.8 psum.24
  627.1 5.7 all-gather.2.cloned.1.call-done
  632.8 5.3 dynamic-slice_select_fusion.4
  638.2 8.8 convolution_convert_fusion.6
  650.0 7.2 all_gather.25
  657.2 9.6 %select_dynamic-update-slice_fusion.2 = (bf16[512,2048]{1,0:T(8,128)(2,1)}, bf16[64,2048]{1,0:T(8,128)(2,1)S(1)}) fusion(bf16[512,2048]{1,0:T(8,128)(2,1)} %get-tuple-element.624, s32[]{:T(128)S(6)} %select_n.328, pred[]{:T(512)S(6)} %and.146, bf16[64,4096]{1,0:T(8,128)(2,1)S(1)} %bitcast.124, bf16[4096,2048]{1,0:T(8,128)(2,1)} %get-tuple-element.658, ...), kind=kOutput, calls=%fused_computation.27.clone.1 | convolution fusion | flops 1074266112 | bytes 18350084 | tf_op jit(solution)/shard_map/while/body/eval_jaxpr/dot_general | solution.py:118
  684.4 5.8 psum.24
  701.9 5.5 all-gather.2.cloned.1.call-done
  707.4 5.3 dynamic-slice_select_fusion.4
  712.9 8.8 convolution_convert_fusion.6
  724.7 7.2 all_gather.25
  731.9 9.6 %select_dynamic-update-slice_fusion.2 = (bf16[512,2048]{1,0:T(8,128)(2,1)}, bf16[64,2048]{1,0:T(8,128)(2,1)S(1)}) fusion(bf16[512,2048]{1,0:T(8,128)(2,1)} %get-tuple-element.624, s32[]{:T(128)S(6)} %select_n.328, pred[]{:T(512)S(6)} %and.146, bf16[64,4096]{1,0:T(8,128)(2,1)S(1)} %bitcast.124, bf16[4096,2048]{1,0:T(8,128)(2,1)} %get-tuple-element.658, ...), kind=kOutput, calls=%fused_computation.27.clone.1 | convolution fusion | flops 1074266112 | bytes 18350084 | tf_op jit(solution)/shard_map/while/body/eval_jaxpr/dot_general | solution.py:118
  759.0 5.8 psum.24
  787.1 8.8 convolution_convert_fusion.6
  798.9 7.2 all_gather.25
  806.1 9.6 %select_dynamic-update-slice_fusion.2 = (bf16[512,2048]{1,0:T(8,128)(2,1)}, bf16[64,2048]{1,0:T(8,128)(2,1)S(1)}) fusion(bf16[512,2048]{1,0:T(8,128)(2,1)} %get-tuple-element.624, s32[]{:T(128)S(6)} %select_n.328, pred[]{:T(512)S(6)} %and.146, bf16[64,4096]{1,0:T(8,128)(2,1)S(1)} %bitcast.124, bf16[4096,2048]{1,0:T(8,128)(2,1)} %get-tuple-element.658, ...), kind=kOutput, calls=%fused_computation.27.clone.1 | convolution fusion | flops 1074266112 | bytes 18350084 | tf_op jit(solution)/shard_map/while/body/eval_jaxpr/dot_general | solution.py:118
  833.7 86.3 %all-reduce.2.cloned.1.call-done = bf16[512,2048]{1,0:T(8,128)(2,1)} async-done(((bf16[512,2048]{1,0:T(8,128)(2,1)}), bf16[512,2048]{1,0:T(8,128)(2,1)}) %all-reduce.2.cloned.1.call-update) | async-done | bytes 2097168 | tf_op jit(solution)/shard_map/psum | solution.py:28
  (590 shorter events, 378.5 us)
Async XLA Ops:
  8.0 1.8 copy-start.2
  8.0 1.8 copy-start.3
  9.8 27.7 %all-gather.2.cloned.1.call-start = ((), (), s32[]{:S(2)}) async-start(), calls=%async_computation.3 | async-start | bytes 1310720 | tf_op jit(solution)/shard_map/while/body/eval_jaxpr/all_gather | solution.py:134
  23.0 6.9 all-to-all-start
  37.5 5.5 copy-start
  71.2 16.3 %collective-permute-start = (bf16[64,2048]{1,0:T(8,128)(2,1)S(1)}, bf16[64,2048]{1,0:T(8,128)(2,1)S(1)}, u32[]{:S(2)}, u32[]{:S(2)}) collective-permute-start(bf16[64,2048]{1,0:T(8,128)(2,1)S(1)} %get-tuple-element.589), channel_id=1, source_target_pairs={{0,1},{1,2},{2,3},{4,5},{5,6},{6,7},{8,9},{9,10},{10,11},{12,13},{... | collective-permute-start | bytes 786440 | tf_op jit(solution)/shard_map/while/body/eval_jaxpr/ppermute | solution.py:23
  76.1 7.9 all-to-all-start.1
  87.5 24.3 %all-gather.2.cloned.1.call-start = ((), (), s32[]{:S(2)}) async-start(), calls=%async_computation.3 | async-start | bytes 1310720 | tf_op jit(solution)/shard_map/while/body/eval_jaxpr/all_gather | solution.py:134
  98.1 6.9 all-to-all-start
  111.9 5.5 copy-start
  146.0 15.9 %collective-permute-start = (bf16[64,2048]{1,0:T(8,128)(2,1)S(1)}, bf16[64,2048]{1,0:T(8,128)(2,1)S(1)}, u32[]{:S(2)}, u32[]{:S(2)}) collective-permute-start(bf16[64,2048]{1,0:T(8,128)(2,1)S(1)} %get-tuple-element.589), channel_id=1, source_target_pairs={{0,1},{1,2},{2,3},{4,5},{5,6},{6,7},{8,9},{9,10},{10,11},{12,13},{... | collective-permute-start | bytes 786440 | tf_op jit(solution)/shard_map/while/body/eval_jaxpr/ppermute | solution.py:23
  150.4 7.9 all-to-all-start.1
  161.9 24.3 %all-gather.2.cloned.1.call-start = ((), (), s32[]{:S(2)}) async-start(), calls=%async_computation.3 | async-start | bytes 1310720 | tf_op jit(solution)/shard_map/while/body/eval_jaxpr/all_gather | solution.py:134
  172.4 6.9 all-to-all-start
  186.2 5.5 copy-start
  219.9 16.7 %collective-permute-start = (bf16[64,2048]{1,0:T(8,128)(2,1)S(1)}, bf16[64,2048]{1,0:T(8,128)(2,1)S(1)}, u32[]{:S(2)}, u32[]{:S(2)}) collective-permute-start(bf16[64,2048]{1,0:T(8,128)(2,1)S(1)} %get-tuple-element.589), channel_id=1, source_target_pairs={{0,1},{1,2},{2,3},{4,5},{5,6},{6,7},{8,9},{9,10},{10,11},{12,13},{... | collective-permute-start | bytes 786440 | tf_op jit(solution)/shard_map/while/body/eval_jaxpr/ppermute | solution.py:23
  225.2 7.9 all-to-all-start.1
  236.7 23.8 %all-gather.2.cloned.1.call-start = ((), (), s32[]{:S(2)}) async-start(), calls=%async_computation.3 | async-start | bytes 1310720 | tf_op jit(solution)/shard_map/while/body/eval_jaxpr/all_gather | solution.py:134
  247.2 6.9 all-to-all-start
  260.5 5.5 copy-start
  294.6 15.8 %collective-permute-start = (bf16[64,2048]{1,0:T(8,128)(2,1)S(1)}, bf16[64,2048]{1,0:T(8,128)(2,1)S(1)}, u32[]{:S(2)}, u32[]{:S(2)}) collective-permute-start(bf16[64,2048]{1,0:T(8,128)(2,1)S(1)} %get-tuple-element.589), channel_id=1, source_target_pairs={{0,1},{1,2},{2,3},{4,5},{5,6},{6,7},{8,9},{9,10},{10,11},{12,13},{... | collective-permute-start | bytes 786440 | tf_op jit(solution)/shard_map/while/body/eval_jaxpr/ppermute | solution.py:23
  299.0 7.9 all-to-all-start.1
  310.5 24.3 %all-gather.2.cloned.1.call-start = ((), (), s32[]{:S(2)}) async-start(), calls=%async_computation.3 | async-start | bytes 1310720 | tf_op jit(solution)/shard_map/while/body/eval_jaxpr/all_gather | solution.py:134
  321.0 6.9 all-to-all-start
  334.8 5.5 copy-start
  368.5 16.7 %collective-permute-start = (bf16[64,2048]{1,0:T(8,128)(2,1)S(1)}, bf16[64,2048]{1,0:T(8,128)(2,1)S(1)}, u32[]{:S(2)}, u32[]{:S(2)}) collective-permute-start(bf16[64,2048]{1,0:T(8,128)(2,1)S(1)} %get-tuple-element.589), channel_id=1, source_target_pairs={{0,1},{1,2},{2,3},{4,5},{5,6},{6,7},{8,9},{9,10},{10,11},{12,13},{... | collective-permute-start | bytes 786440 | tf_op jit(solution)/shard_map/while/body/eval_jaxpr/ppermute | solution.py:23
  373.8 7.9 all-to-all-start.1
  385.3 24.3 %all-gather.2.cloned.1.call-start = ((), (), s32[]{:S(2)}) async-start(), calls=%async_computation.3 | async-start | bytes 1310720 | tf_op jit(solution)/shard_map/while/body/eval_jaxpr/all_gather | solution.py:134
  395.8 6.9 all-to-all-start
  409.5 5.5 copy-start
  443.6 15.9 %collective-permute-start = (bf16[64,2048]{1,0:T(8,128)(2,1)S(1)}, bf16[64,2048]{1,0:T(8,128)(2,1)S(1)}, u32[]{:S(2)}, u32[]{:S(2)}) collective-permute-start(bf16[64,2048]{1,0:T(8,128)(2,1)S(1)} %get-tuple-element.589), channel_id=1, source_target_pairs={{0,1},{1,2},{2,3},{4,5},{5,6},{6,7},{8,9},{9,10},{10,11},{12,13},{... | collective-permute-start | bytes 786440 | tf_op jit(solution)/shard_map/while/body/eval_jaxpr/ppermute | solution.py:23
  448.1 7.9 all-to-all-start.1
  459.5 24.2 %all-gather.2.cloned.1.call-start = ((), (), s32[]{:S(2)}) async-start(), calls=%async_computation.3 | async-start | bytes 1310720 | tf_op jit(solution)/shard_map/while/body/eval_jaxpr/all_gather | solution.py:134
  470.0 6.9 all-to-all-start
  483.8 5.5 copy-start
  517.4 16.8 %collective-permute-start = (bf16[64,2048]{1,0:T(8,128)(2,1)S(1)}, bf16[64,2048]{1,0:T(8,128)(2,1)S(1)}, u32[]{:S(2)}, u32[]{:S(2)}) collective-permute-start(bf16[64,2048]{1,0:T(8,128)(2,1)S(1)} %get-tuple-element.589), channel_id=1, source_target_pairs={{0,1},{1,2},{2,3},{4,5},{5,6},{6,7},{8,9},{9,10},{10,11},{12,13},{... | collective-permute-start | bytes 786440 | tf_op jit(solution)/shard_map/while/body/eval_jaxpr/ppermute | solution.py:23
  522.8 7.9 all-to-all-start.1
  534.2 24.2 %all-gather.2.cloned.1.call-start = ((), (), s32[]{:S(2)}) async-start(), calls=%async_computation.3 | async-start | bytes 1310720 | tf_op jit(solution)/shard_map/while/body/eval_jaxpr/all_gather | solution.py:134
  544.8 6.9 all-to-all-start
  558.5 5.5 copy-start
  592.5 15.9 %collective-permute-start = (bf16[64,2048]{1,0:T(8,128)(2,1)S(1)}, bf16[64,2048]{1,0:T(8,128)(2,1)S(1)}, u32[]{:S(2)}, u32[]{:S(2)}) collective-permute-start(bf16[64,2048]{1,0:T(8,128)(2,1)S(1)} %get-tuple-element.589), channel_id=1, source_target_pairs={{0,1},{1,2},{2,3},{4,5},{5,6},{6,7},{8,9},{9,10},{10,11},{12,13},{... | collective-permute-start | bytes 786440 | tf_op jit(solution)/shard_map/while/body/eval_jaxpr/ppermute | solution.py:23
  596.9 7.9 all-to-all-start.1
  608.4 24.3 %all-gather.2.cloned.1.call-start = ((), (), s32[]{:S(2)}) async-start(), calls=%async_computation.3 | async-start | bytes 1310720 | tf_op jit(solution)/shard_map/while/body/eval_jaxpr/all_gather | solution.py:134
  618.9 6.9 all-to-all-start
  632.8 5.5 copy-start
  666.8 16.4 %collective-permute-start = (bf16[64,2048]{1,0:T(8,128)(2,1)S(1)}, bf16[64,2048]{1,0:T(8,128)(2,1)S(1)}, u32[]{:S(2)}, u32[]{:S(2)}) collective-permute-start(bf16[64,2048]{1,0:T(8,128)(2,1)S(1)} %get-tuple-element.589), channel_id=1, source_target_pairs={{0,1},{1,2},{2,3},{4,5},{5,6},{6,7},{8,9},{9,10},{10,11},{12,13},{... | collective-permute-start | bytes 786440 | tf_op jit(solution)/shard_map/while/body/eval_jaxpr/ppermute | solution.py:23
  671.7 7.9 all-to-all-start.1
  683.2 24.2 %all-gather.2.cloned.1.call-start = ((), (), s32[]{:S(2)}) async-start(), calls=%async_computation.3 | async-start | bytes 1310720 | tf_op jit(solution)/shard_map/while/body/eval_jaxpr/all_gather | solution.py:134
  693.7 6.9 all-to-all-start
  707.4 5.5 copy-start
  741.4 16.4 %collective-permute-start = (bf16[64,2048]{1,0:T(8,128)(2,1)S(1)}, bf16[64,2048]{1,0:T(8,128)(2,1)S(1)}, u32[]{:S(2)}, u32[]{:S(2)}) collective-permute-start(bf16[64,2048]{1,0:T(8,128)(2,1)S(1)} %get-tuple-element.589), channel_id=1, source_target_pairs={{0,1},{1,2},{2,3},{4,5},{5,6},{6,7},{8,9},{9,10},{10,11},{12,13},{... | collective-permute-start | bytes 786440 | tf_op jit(solution)/shard_map/while/body/eval_jaxpr/ppermute | solution.py:23
  746.3 7.9 all-to-all-start.1
  757.8 23.8 %all-gather.2.cloned.1.call-start = ((), (), s32[]{:S(2)}) async-start(), calls=%async_computation.3 | async-start | bytes 1310720 | tf_op jit(solution)/shard_map/while/body/eval_jaxpr/all_gather | solution.py:134
  768.3 6.9 all-to-all-start
  781.6 5.5 copy-start
  815.7 16.4 %collective-permute-start = (bf16[64,2048]{1,0:T(8,128)(2,1)S(1)}, bf16[64,2048]{1,0:T(8,128)(2,1)S(1)}, u32[]{:S(2)}, u32[]{:S(2)}) collective-permute-start(bf16[64,2048]{1,0:T(8,128)(2,1)S(1)} %get-tuple-element.589), channel_id=1, source_target_pairs={{0,1},{1,2},{2,3},{4,5},{5,6},{6,7},{8,9},{9,10},{10,11},{12,13},{... | collective-permute-start | bytes 786440 | tf_op jit(solution)/shard_map/while/body/eval_jaxpr/ppermute | solution.py:23
  820.5 7.9 all-to-all-start.1
  832.1 1.6 copy-start.1
  832.1 87.9 %all-reduce.2.cloned.1.call-start = ((), (), s32[]{:S(2)}) async-start(), calls=%async_computation.2 | async-start | bytes 4194304 | tf_op jit(solution)/shard_map/psum | solution.py:28
Sparse Core Ops, SparseCore 0:
  20.5 17.0 all-gather.1
  95.6 16.2 all-gather.1
  169.9 16.2 all-gather.1
  244.7 15.7 all-gather.1
  318.5 16.2 all-gather.1
  393.2 16.2 all-gather.1
  467.5 16.2 all-gather.1
  542.3 16.1 all-gather.1
  616.4 16.3 all-gather.1
  691.2 16.1 all-gather.1
  765.8 15.7 all-gather.1
Sparse Core Ops, SparseCore 1:
  834.9 85.0 all-reduce.1
